TPU v7x, 32 devices: a whole 2x2x4 slice. The times are simulated.
32 devices in a mesh: dp: 2 (over x), ei: 4 (over z), eo: 4 (over y, core).
Axes of the slice: x: 2, y: 2, z: 4, core: 2. Of those that a mesh axis runs over, the one named last changes fastest.
Arguments:
- x: bfloat16 [131072, 1024], P(('dp', 'ei', 'eo')), parts along dimension 0
- slots: int32 [1024, 256], P(('dp', 'ei', 'eo')), parts along dimension 0
- gates: float32 [131072, 2], P(('dp', 'ei', 'eo')), parts along dimension 0
- w1: bfloat16 [32, 1024, 512], P(('ei', 'eo'))
- w3: bfloat16 [32, 1024, 512], P(('ei', 'eo'))
- w2: bfloat16 [32, 512, 1024], P(('ei', 'eo'))
- dy: bfloat16 [131072, 1024], P(('dp', 'ei', 'eo')), parts along dimension 0
Outputs:
- output 1: bfloat16 [131072, 1024], P(('dp', 'ei', 'eo')), parts along dimension 0
- output 2: bfloat16 [131072, 1024], P(('dp', 'ei', 'eo')), parts along dimension 0
- output 3: float32 [131072, 2], P(('dp', 'ei', 'eo')), parts along dimension 0
- output 4: float32 [64, 1024, 512], P(('dp', 'ei', 'eo')), parts along dimension 0
- output 5: float32 [64, 1024, 512], P(('dp', 'ei', 'eo')), parts along dimension 0
- output 6: float32 [64, 512, 1024], P(('dp', 'ei', 'eo')), parts along dimension 0
There are 2 independent parts. A program takes and returns all parts, laid end to end along the dimension named above; an argument that names none is the same for every part.
All inputs are finite; a program needn't handle non-finite values.
Results may differ from a plain program's by a relative error of at most 0.001.
Values are sent between devices in bfloat16 or wider.
A program may use at most 1 GiB of HBM per device.

v0:
```python
import jax
import jax.numpy as jnp
from jax import lax
from jax.sharding import PartitionSpec as P, NamedSharding


def _fwd(xr, w1, w3, w2):
    a = jnp.einsum('ecd,edf->ecf', xr, w1, preferred_element_type=jnp.float32)
    b = jnp.einsum('ecd,edf->ecf', xr, w3, preferred_element_type=jnp.float32)
    h = (a * jax.nn.sigmoid(a) * b).astype(jnp.bfloat16)
    o = jnp.einsum('ecf,efd->ecd', h, w2, preferred_element_type=jnp.float32).astype(jnp.bfloat16)
    return a, b, h, o


def _bwd(xr, a, b, h, do, w1, w3, w2):
    sg = jax.nn.sigmoid(a)
    dh = jnp.einsum('ecd,efd->ecf', do, w2, preferred_element_type=jnp.float32)
    da = (dh * b * (sg * (1.0 + a * (1.0 - sg)))).astype(jnp.bfloat16)
    db = (dh * (a * sg)).astype(jnp.bfloat16)
    dx = (jnp.einsum('ecf,edf->ecd', da, w1, preferred_element_type=jnp.float32)
          + jnp.einsum('ecf,edf->ecd', db, w3, preferred_element_type=jnp.float32)).astype(jnp.bfloat16)
    dw1 = jnp.einsum('ecd,ecf->edf', xr, da, preferred_element_type=jnp.float32)
    dw3 = jnp.einsum('ecd,ecf->edf', xr, db, preferred_element_type=jnp.float32)
    dw2 = jnp.einsum('ecf,ecd->efd', h, do, preferred_element_type=jnp.float32)
    return dx, dw1, dw3, dw2


def solution(mesh):
    n_i = mesh.shape['ei']
    n_o = mesh.shape['eo']
    grp = n_i * n_o
    tok = P(('dp', 'ei', 'eo'), None)
    wsp = P(('ei', 'eo'), None, None)
    dwsp = P(('dp', 'ei', 'eo'), None, None)

    def to_experts(buf):
        n_exp, cap, d = buf.shape
        el = n_exp // grp
        r = buf.reshape(n_i, n_o, el, cap, d)
        r = lax.all_to_all(r, 'eo', 1, 1, tiled=True)
        r = lax.all_to_all(r, 'ei', 0, 0, tiled=True)
        return r.transpose(2, 0, 1, 3, 4).reshape(el, grp * cap, d)

    def to_sources(rows, cap):
        el, _, d = rows.shape
        r = rows.reshape(el, n_i, n_o, cap, d).transpose(1, 2, 0, 3, 4)
        r = lax.all_to_all(r, 'ei', 0, 0, tiled=True)
        r = lax.all_to_all(r, 'eo', 1, 1, tiled=True)
        return r.reshape(grp * el * cap, d)

    def local(x, slots, gates, w1, w3, w2, dy):
        t, d = x.shape
        k = gates.shape[1]
        n_exp, cap = slots.shape
        nk = t * k
        flat = slots.reshape(-1)
        valid = flat < nk
        mc = jnp.minimum(flat, nk - 1)
        rows = mc // k
        xb = jnp.where(valid[:, None], x[rows], jnp.zeros((), x.dtype)).reshape(n_exp, cap, d)
        xr = to_experts(xb)
        a, b, h, o = _fwd(xr, w1, w3, w2)
        ob = to_sources(o, cap)
        pos = jnp.zeros((nk + 1,), jnp.int32).at[flat].set(jnp.arange(n_exp * cap, dtype=jnp.int32))[:nk]
        oa = ob[pos].reshape(t, k, d)
        y = jnp.sum(gates[:, :, None] * oa.astype(jnp.float32), axis=1).astype(jnp.bfloat16)
        dgates = jnp.einsum('tkd,td->tk', oa, dy, preferred_element_type=jnp.float32)
        gs = jnp.where(valid, gates.reshape(-1)[mc], 0.0)
        dob = (gs[:, None] * dy[rows].astype(jnp.float32)).astype(jnp.bfloat16).reshape(n_exp, cap, d)
        dor = to_experts(dob)
        dxr, dw1, dw3, dw2 = _bwd(xr, a, b, h, dor, w1, w3, w2)
        dxb = to_sources(dxr, cap)
        dxa = dxb[pos].reshape(t, k, d)
        dx = jnp.sum(dxa.astype(jnp.float32), axis=1).astype(jnp.bfloat16)
        return y, dx, dgates, dw1, dw3, dw2

    return jax.shard_map(local, mesh=mesh, in_specs=(tok, tok, tok, wsp, wsp, wsp, tok),
                         out_specs=(tok, tok, tok, dwsp, dwsp, dwsp), check_vma=False)
```

profile of v0, /device:TPU:0, one launch (start us, length us, event | category | flops | bytes accessed | tf_op | source)
XLA Modules:
  0.0 2650.7 jit_solution(4426004217139327034)
XLA Ops:
  8.7 45.5 %gather_fusion.2 = f32[8192]{0:T(1024)S(1)} fusion(f32[8192]{0:T(1024)S(1)} %reshape.178, s32[8192]{0:T(1024)S(1)} %broadcast_clamp_fusion), kind=kCustom, calls=%fused_computation.2 | custom fusion | bytes 98304 | tf_op jit(solution)/shard_map/gather | solution.py:68
  54.3 45.3 %gather_fusion.3 = bf16[8192,1024]{1,0:T(8,128)(2,1)} fusion(bf16[4096,1024]{1,0:T(8,128)(2,1)} %param.13, s32[8192]{0:T(1024)S(1)} %broadcast_clamp_fusion.1), kind=kCustom, calls=%fused_computation.3 | custom fusion | bytes 33587200 | tf_op jit(solution)/shard_map/gather | solution.py:69
  99.6 14.6 fusion
  114.3 7.0 all-to-all-start.4
  121.3 45.1 %gather_fusion = bf16[8192,1024]{1,0:T(8,128)(2,1)} fusion(bf16[4096,1024]{1,0:T(8,128)(2,1)} %param.7, s32[8192]{0:T(1024)S(1)} %broadcast_clamp_fusion.1), kind=kCustom, calls=%fused_computation | custom fusion | bytes 33587200 | tf_op jit(solution)/shard_map/gather | solution.py:60
  166.4 14.0 copy_select_fusion
  180.4 124.2 %all-to-all-done.4 = bf16[4,4,2,256,1024]{4,3,0,2,1:T(8,128)(2,1)} async-done(((bf16[4,4,2,256,1024]{4,3,0,2,1:T(8,128)(2,1)}), bf16[4,4,2,256,1024]{4,3,0,2,1:T(8,128)(2,1)}, u32[]{:S(2)}, u32[]{:S(2)}) %all-to-all-start.4) | async-done | bytes 16777248 | tf_op jit(solution)/shard_map/all_to_all | solution.py:40
  304.7 7.0 all-to-all-start
  311.7 13.9 copy.45
  325.6 168.8 %all-to-all-done = bf16[4,4,2,256,1024]{4,3,0,2,1:T(8,128)(2,1)} async-done(((bf16[4,4,2,256,1024]{4,3,0,2,1:T(8,128)(2,1)}), bf16[4,4,2,256,1024]{4,3,0,2,1:T(8,128)(2,1)}, u32[]{:S(2)}, u32[]{:S(2)}) %all-to-all-start) | async-done | bytes 16777248 | tf_op jit(solution)/shard_map/all_to_all | solution.py:40
  494.4 7.0 all-to-all-start.5
  501.4 13.9 copy.37
  515.2 349.4 %all-to-all-done.5 = bf16[4,4,2,256,1024]{4,3,1,2,0:T(8,128)(2,1)} async-done(((bf16[4,4,2,256,1024]{4,3,1,2,0:T(8,128)(2,1)}), bf16[4,4,2,256,1024]{4,3,1,2,0:T(8,128)(2,1)}, u32[]{:S(2)}, u32[]{:S(2)}) %all-to-all-start.5) | async-done | bytes 16777248 | tf_op jit(solution)/shard_map/all_to_all | solution.py:41
  864.7 7.3 all-to-all-start.1
  871.9 13.8 copy.46
  885.8 348.2 %all-to-all-done.1 = bf16[4,4,2,256,1024]{4,3,1,2,0:T(8,128)(2,1)} async-done(((bf16[4,4,2,256,1024]{4,3,1,2,0:T(8,128)(2,1)}), bf16[4,4,2,256,1024]{4,3,1,2,0:T(8,128)(2,1)}, u32[]{:S(2)}, u32[]{:S(2)}) %all-to-all-start.1) | async-done | bytes 16777248 | tf_op jit(solution)/shard_map/all_to_all | solution.py:41
  1233.9 13.8 copy.38
  1247.8 18.5 fusion.8
  1266.3 18.5 fusion.7
  1284.8 31.0 %multiply_convert_fusion = (bf16[2,4096,512]{2,1,0:T(8,128)(2,1)}, bf16[2,4096,512]{2,1,0:T(8,128)(2,1)}, bf16[2,4096,512]{2,1,0:T(8,128)(2,1)}) fusion(f32[2,4096,512]{2,1,0:T(8,128)} %fusion.7, f32[2,4096,512]{2,1,0:T(8,128)} %fusion.8, bf16[2,4096,1024]{2,1,0:T(8,128)(2,1)} %bitcast.53, bf16[2,512,1024]{2,1,0:T(8,128)(2,1)S(1)} %copy-done), kind=kOutput, calls=%fused_computation.13 | convolution fusion | flops 8652849152 | bytes 77594624 | tf_op jit(solution)/shard_map/ecd,efd->ecf/dot_general | solution.py:17
  1315.8 15.8 convolution_convert_fusion
  1331.6 13.9 copy.68
  1345.5 7.3 all-to-all-start.2
  1352.8 18.8 fusion.9
  1371.5 23.5 add_convert_fusion
  1395.1 13.8 copy.67
  1408.9 306.0 %all-to-all-done.2 = bf16[4,4,2,256,1024]{4,3,1,2,0:T(8,128)(2,1)} async-done(((bf16[4,4,2,256,1024]{4,3,1,2,0:T(8,128)(2,1)}), bf16[4,4,2,256,1024]{4,3,1,2,0:T(8,128)(2,1)}, u32[]{:S(2)}, u32[]{:S(2)}) %all-to-all-start.2) | async-done | bytes 16777248 | tf_op jit(solution)/shard_map/all_to_all | solution.py:47
  1714.9 7.0 all-to-all-start.6
  1721.9 13.9 copy.40
  1735.8 348.2 %all-to-all-done.6 = bf16[4,4,2,256,1024]{4,3,1,2,0:T(8,128)(2,1)} async-done(((bf16[4,4,2,256,1024]{4,3,1,2,0:T(8,128)(2,1)}), bf16[4,4,2,256,1024]{4,3,1,2,0:T(8,128)(2,1)}, u32[]{:S(2)}, u32[]{:S(2)}) %all-to-all-start.6) | async-done | bytes 16777248 | tf_op jit(solution)/shard_map/all_to_all | solution.py:47
  2084.0 7.0 all-to-all-start.3
  2091.0 30.6 %scatter_custom_fusion = s32[8193]{0:T(1024)S(1)} fusion(s32[8192]{0:T(1024)} %bitcast.66, s32[8192]{0:T(1024)S(1)} %iota.3, s32[]{:T(128)} %constant.24.clone.1), kind=kCustom, calls=%fused_computation.30 | custom fusion | bytes 33284 | tf_op jit(solution)/shard_map/scatter | solution.py:64
  2121.7 13.9 copy.48
  2135.5 138.2 %all-to-all-done.3 = bf16[4,4,2,256,1024]{4,3,0,2,1:T(8,128)(2,1)} async-done(((bf16[4,4,2,256,1024]{4,3,0,2,1:T(8,128)(2,1)}), bf16[4,4,2,256,1024]{4,3,0,2,1:T(8,128)(2,1)}, u32[]{:S(2)}, u32[]{:S(2)}) %all-to-all-start.3) | async-done | bytes 16777248 | tf_op jit(solution)/shard_map/all_to_all | solution.py:48
  2273.7 7.2 all-to-all-start.7
  2280.9 16.2 fusion.11
  2297.1 16.2 fusion.10
  2313.3 16.6 fusion.12
  2329.8 13.8 copy.41
  2343.6 48.6 %gather_fusion.1 = bf16[8192,1024]{1,0:T(8,128)(2,1)} fusion(bf16[8192,1024]{1,0:T(8,128)(2,1)} %bitcast.48, s32[8192]{0:T(1024)S(1)} %fusion.4), kind=kCustom, calls=%fused_computation.1 | custom fusion | bytes 33587200 | tf_op jit(solution)/shard_map/gather | solution.py:65
  2392.2 24.9 reshape.177
  2417.2 42.4 %fusion.2 = f32[4096,1,2]{2,1,0:T(1,128)} fusion(bf16[4096,2,1024]{2,1,0:T(2,128)(2,1)} %reshape.177, bf16[4096,1024,1]{1,0,2:T(8,128)(2,1)} %bitcast.46), kind=kOutput, calls=%fused_computation.18 | convolution fusion | flops 16777216 | bytes 25198592 | tf_op jit(solution)/shard_map/tkd,td->tk/dot_general | solution.py:67
  2459.5 5.1 copy.54
  2464.6 52.3 %multiply_reduce_fusion = bf16[4096,1024]{1,0:T(8,128)(2,1)} fusion(bf16[4096,2,1024]{2,1,0:T(2,128)(2,1)} %reshape.177, f32[4096,2]{1,0:T(8,128)S(1)} %copy-done.2), kind=kLoop, calls=%fused_computation.9 | loop fusion | flops 20971520 | bytes 25198592 | tf_op jit(solution)/shard_map/reduce_sum | solution.py:66
  2516.9 13.8 copy.49
  2530.7 48.7 %gather_fusion.4 = bf16[8192,1024]{1,0:T(8,128)(2,1)} fusion(bf16[8192,1024]{1,0:T(8,128)(2,1)} %bitcast.47, s32[8192]{0:T(1024)S(1)} %fusion.4), kind=kCustom, calls=%fused_computation.4 | custom fusion | bytes 33587200 | tf_op jit(solution)/shard_map/gather | solution.py:73
  2579.5 25.1 reshape.182
  2604.6 46.0 %reduce_sum.22 = bf16[4096,1024]{1,0:T(8,128)(2,1)} reduce(bf16[4096,2,1024]{2,1,0:T(2,128)(2,1)} %reshape.182, bf16[]{:T(256)} %constant.27.clone.1), dimensions={1}, to_apply=%region_2.3 | reduce | flops 4194304 | bytes 25165826 | tf_op jit(solution)/shard_map/reduce_sum | solution.py:74
  (23 shorter events, 8.2 us)
Async XLA Ops:
  0.6 1284.2 %copy-start = (bf16[2,512,1024]{2,1,0:T(8,128)(2,1)S(1)}, bf16[2,512,1024]{2,1,0:T(8,128)(2,1)}, u32[]{:S(2)}) copy-start(bf16[2,512,1024]{2,1,0:T(8,128)(2,1)} %param.12) | copy-start | bytes 6291460
  114.3 190.4 %all-to-all-start.4 = ((bf16[4,4,2,256,1024]{4,3,0,2,1:T(8,128)(2,1)}), bf16[4,4,2,256,1024]{4,3,0,2,1:T(8,128)(2,1)}, u32[]{:S(2)}, u32[]{:S(2)}) async-start(bf16[4,4,2,256,1024]{4,3,0,2,1:T(8,128)(2,1)} %fusion), calls=%async_computation.4 | async-start | bytes 33554432 | tf_op jit(solution)/shard_map/all_to_all | solution.py:40
  304.7 189.7 %all-to-all-start = ((bf16[4,4,2,256,1024]{4,3,0,2,1:T(8,128)(2,1)}), bf16[4,4,2,256,1024]{4,3,0,2,1:T(8,128)(2,1)}, u32[]{:S(2)}, u32[]{:S(2)}) async-start(bf16[4,4,2,256,1024]{4,3,0,2,1:T(8,128)(2,1)} %copy_select_fusion), calls=%async_computation | async-start | bytes 33554432 | tf_op jit(solution)/shard_map/all_to_all | solution.py:40
  494.4 370.3 %all-to-all-start.5 = ((bf16[4,4,2,256,1024]{4,3,1,2,0:T(8,128)(2,1)}), bf16[4,4,2,256,1024]{4,3,1,2,0:T(8,128)(2,1)}, u32[]{:S(2)}, u32[]{:S(2)}) async-start(bf16[4,4,2,256,1024]{4,3,1,2,0:T(8,128)(2,1)} %copy.45), calls=%async_computation.5 | async-start | bytes 33554432 | tf_op jit(solution)/shard_map/all_to_all | solution.py:41
  864.7 369.3 %all-to-all-start.1 = ((bf16[4,4,2,256,1024]{4,3,1,2,0:T(8,128)(2,1)}), bf16[4,4,2,256,1024]{4,3,1,2,0:T(8,128)(2,1)}, u32[]{:S(2)}, u32[]{:S(2)}) async-start(bf16[4,4,2,256,1024]{4,3,1,2,0:T(8,128)(2,1)} %copy.37), calls=%async_computation.1 | async-start | bytes 33554432 | tf_op jit(solution)/shard_map/all_to_all | solution.py:41
  1345.5 7.3 copy-start.3
  1345.5 369.4 %all-to-all-start.2 = ((bf16[4,4,2,256,1024]{4,3,1,2,0:T(8,128)(2,1)}), bf16[4,4,2,256,1024]{4,3,1,2,0:T(8,128)(2,1)}, u32[]{:S(2)}, u32[]{:S(2)}) async-start(bf16[4,4,2,256,1024]{4,3,1,2,0:T(8,128)(2,1)} %bitcast.52), calls=%async_computation.2 | async-start | bytes 33554432 | tf_op jit(solution)/shard_map/all_to_all | solution.py:47
  1714.9 369.1 %all-to-all-start.6 = ((bf16[4,4,2,256,1024]{4,3,1,2,0:T(8,128)(2,1)}), bf16[4,4,2,256,1024]{4,3,1,2,0:T(8,128)(2,1)}, u32[]{:S(2)}, u32[]{:S(2)}) async-start(bf16[4,4,2,256,1024]{4,3,1,2,0:T(8,128)(2,1)} %bitcast.51), calls=%async_computation.6 | async-start | bytes 33554432 | tf_op jit(solution)/shard_map/all_to_all | solution.py:47
  2084.0 189.7 %all-to-all-start.3 = ((bf16[4,4,2,256,1024]{4,3,0,2,1:T(8,128)(2,1)}), bf16[4,4,2,256,1024]{4,3,0,2,1:T(8,128)(2,1)}, u32[]{:S(2)}, u32[]{:S(2)}) async-start(bf16[4,4,2,256,1024]{4,3,0,2,1:T(8,128)(2,1)} %copy.40), calls=%async_computation.3 | async-start | bytes 33554432 | tf_op jit(solution)/shard_map/all_to_all | solution.py:48
  2273.7 243.2 %all-to-all-start.7 = ((bf16[4,4,2,256,1024]{4,3,0,2,1:T(8,128)(2,1)}), bf16[4,4,2,256,1024]{4,3,0,2,1:T(8,128)(2,1)}, u32[]{:S(2)}, u32[]{:S(2)}) async-start(bf16[4,4,2,256,1024]{4,3,0,2,1:T(8,128)(2,1)} %copy.48), calls=%async_computation.7 | async-start | bytes 33554432 | tf_op jit(solution)/shard_map/all_to_all | solution.py:48
  2417.2 47.5 %copy-start.2 = (f32[4096,2]{1,0:T(8,128)S(1)}, f32[4096,2]{1,0:T(8,128)}, u32[]{:S(2)}) copy-start(f32[4096,2]{1,0:T(8,128)} %copy.34) | copy-start | bytes 98308
  2579.5 71.0 %copy-start.1 = (bf16[2,512,1024]{2,1,0:T(8,128)(2,1)S(1)}, bf16[2,512,1024]{2,1,0:T(8,128)(2,1)}, u32[]{:S(2)}) copy-start(bf16[2,512,1024]{2,1,0:T(8,128)(2,1)} %param.12) | copy-start | bytes 6291460
where the time goes:
time: 2660 us; the launch traced here: 2650 us
  waiting for transfers between devices  1780 us (67%)
  local copies, waits for them, and re-layouts  464 us (17%)
  matrix products  217 us (8%)
  other arithmetic  129 us (5%)
  starting transfers between devices  56.7 us (2%)
    all_to_all x2, waiting for transfers between devices, to_experts(): r = lax.all_to_all(r, 'ei', 0, 0, tiled=True)  698 us
    all_to_all x2, waiting for transfers between devices, to_sources(): r = lax.all_to_all(r, 'ei', 0, 0, tiled=True)  654 us
    all_to_all x2, waiting for transfers between devices, to_experts(): r = lax.all_to_all(r, 'eo', 1, 1, tiled=True)  293 us
    all_to_all x2, waiting for transfers between devices, to_sources(): r = lax.all_to_all(r, 'eo', 1, 1, tiled=True)  138 us
  transfers between devices with their start and end apart: 8, of which 7 were waited for; matrix products, arithmetic and copies ran while one was open for 17% of the time, Pallas kernels for 0%

commit v1 on v0

v1 whole, which is shorter than its diff:
```python
import functools
import jax
import jax.numpy as jnp
from jax import lax
from jax.experimental import pallas as pl
from jax.experimental.pallas import tpu as pltpu
from jax.sharding import PartitionSpec as P

F32 = jnp.float32
BF16 = jnp.bfloat16


def _dot(a, b, ca, cb):
    return lax.dot_general(a, b, (((ca,), (cb,)), ((), ())), preferred_element_type=F32)


def _expert_kernel(tile, x_ref, do_ref, w1_ref, w3_ref, w2_ref, *rest):
    o_ref, dx_ref, dw1_ref, dw3_ref, dw2_ref, h_s, da_s, db_s = rest[-8:]
    n_o, _, cap, d = x_ref.shape
    rows = n_o * cap
    w1 = w1_ref[0]
    w3 = w3_ref[0]
    w2 = w2_ref[0]
    per = tile // cap
    for r in range(rows // tile):
        xs = x_ref[r * per:(r + 1) * per, 0].reshape(tile, d)
        dos = do_ref[r * per:(r + 1) * per, 0].reshape(tile, d)
        a = _dot(xs, w1, 1, 0)
        b = _dot(xs, w3, 1, 0)
        sg = jax.nn.sigmoid(a)
        s = a * sg
        h = (s * b).astype(BF16)
        dh = _dot(dos, w2, 1, 1)
        da = (dh * b * (sg * (1.0 + a * (1.0 - sg)))).astype(BF16)
        db = (dh * s).astype(BF16)
        h_s[r * tile:(r + 1) * tile] = h
        da_s[r * tile:(r + 1) * tile] = da
        db_s[r * tile:(r + 1) * tile] = db
        o_ref[r * per:(r + 1) * per, 0, 0] = _dot(h, w2, 1, 0).astype(BF16).reshape(per, cap, d)
        dx = _dot(da, w1, 1, 1) + _dot(db, w3, 1, 1)
        dx_ref[r * per:(r + 1) * per, 0, 0] = dx.astype(BF16).reshape(per, cap, d)
    xa = x_ref[:, 0].reshape(rows, d)
    doa = do_ref[:, 0].reshape(rows, d)
    dw1_ref[0] = _dot(xa, da_s[...], 0, 0)
    dw3_ref[0] = _dot(xa, db_s[...], 0, 0)
    dw2_ref[0] = _dot(h_s[...], doa, 0, 0)


def _experts(c, n_c, x, do, w1, w3, w2, carry):
    n_o, n_i, cap, d = x.shape
    f = w1.shape[2]
    rows = n_o * cap
    tok = pl.BlockSpec((n_o, 1, cap, d), lambda i: (0, i, 0, 0))
    wab = pl.BlockSpec((1, d, f), lambda i: (i, 0, 0))
    wc = pl.BlockSpec((1, f, d), lambda i: (i, 0, 0))
    back = pl.BlockSpec((n_o, 1, 1, cap, d), lambda i: (0, c, i, 0, 0))
    full = jax.ShapeDtypeStruct((n_o, n_c, n_i, cap, d), BF16)
    extra = [] if carry is None else [pl.BlockSpec(memory_space=pl.ANY)] * 2
    alias = {} if carry is None else {5: 0, 6: 1}
    args = (x, do, w1, w3, w2) + (() if carry is None else carry)

    return pl.pallas_call(
        functools.partial(_expert_kernel, 512),
        grid=(n_i,),
        in_specs=[tok, tok, wab, wab, wc] + extra,
        out_specs=[back, back, wab, wab, wc],
        out_shape=[full, full, jax.ShapeDtypeStruct((n_i, d, f), F32), jax.ShapeDtypeStruct((n_i, d, f), F32),
                   jax.ShapeDtypeStruct((n_i, f, d), F32)],
        scratch_shapes=[pltpu.VMEM((rows, f), BF16)] * 3,
        input_output_aliases=alias,
        compiler_params=pltpu.CompilerParams(vmem_limit_bytes=60 * 1024 * 1024),
        cost_estimate=pl.CostEstimate(flops=18 * n_i * rows * d * f, transcendentals=n_i * rows * f,
                                      bytes_accessed=n_i * (8 * rows * d + 18 * d * f)),
        name='experts%d' % c,
    )(*args)


def solution(mesh):
    n_i = mesh.shape['ei']
    n_o = mesh.shape['eo']
    tok = P(('dp', 'ei', 'eo'), None)
    wsp = P(('ei', 'eo'), None, None)
    dwsp = P(('dp', 'ei', 'eo'), None, None)

    def local(x, slots, gates, w1, w3, w2, dy):
        t, d = x.shape
        k = gates.shape[1]
        n_exp, cap = slots.shape
        nk = t * k
        n_c = n_exp // (n_i * n_o)
        sl = slots.reshape(n_i, n_o, n_c, cap).transpose(1, 2, 0, 3)
        flat = sl.reshape(-1)
        gs = jnp.where(flat < nk, gates.reshape(-1)[jnp.minimum(flat, nk - 1)], 0.0)
        gs = gs.reshape(n_o, n_c, n_i, cap)

        xs, dos, ws = [], [], []
        for c in range(n_c):
            idx = (jnp.minimum(sl[:, c], nk - 1) // k).reshape(-1)
            xb = x[idx].reshape(n_o, n_i, cap, d)
            xs.append(lax.all_to_all(xb, 'eo', 0, 0, tiled=True))
            dob = (gs[:, c].reshape(-1)[:, None] * dy[idx].astype(F32)).astype(BF16).reshape(n_o, n_i, cap, d)
            dos.append(lax.all_to_all(dob, 'eo', 0, 0, tiled=True))
            ws.append([lax.all_gather(w[c:c + 1], 'ei', axis=0, tiled=True) for w in (w1, w3, w2)])
        carry = None
        grads = []
        for c in range(n_c):
            o, dx, *dw = _experts(c, n_c, xs[c], dos[c], *ws[c], carry)
            carry = (o, dx)
            grads.append([lax.psum_scatter(g, 'ei', scatter_dimension=0, tiled=True) for g in dw])
        ob = lax.all_to_all(carry[0], 'eo', 0, 0, tiled=True).reshape(n_exp * cap, d)
        dxb = lax.all_to_all(carry[1], 'eo', 0, 0, tiled=True).reshape(n_exp * cap, d)

        pos = jnp.zeros((nk + 1,), jnp.int32).at[flat].set(jnp.arange(n_exp * cap, dtype=jnp.int32))[:nk].reshape(t, k)
        dyf = dy.astype(F32)
        y = 0.0
        dgs = []
        for j in range(k):
            oj = ob[pos[:, j]].astype(F32)
            y = y + gates[:, j:j + 1] * oj
            dgs.append(jnp.sum(dyf * oj, axis=1))
        dgates = jnp.stack(dgs, axis=1)
        dx = 0.0
        for j in range(k):
            dx = dx + dxb[pos[:, j]].astype(F32)
        dw1, dw3, dw2 = (jnp.concatenate([g[q] for g in grads], axis=0) for q in range(3))
        return y.astype(BF16), dx.astype(BF16), dgates, dw1, dw3, dw2

    return jax.shard_map(local, mesh=mesh, in_specs=(tok, tok, tok, wsp, wsp, wsp, tok),
                         out_specs=(tok, tok, tok, dwsp, dwsp, dwsp), check_vma=False)
```

time: 2660 us -> 1440 us (0.54)
  waiting for transfers between devices: 1780 us -> 732 us
  matrix products: 217 us -> 0 us
  blocking collectives: 0 us -> 194 us
  local copies, waits for them, and re-layouts: 464 us -> 311 us
  Pallas kernels: 0 us -> 97.4 us
  other arithmetic: 129 us -> 55.5 us
    all_to_all x8 -> x5, waiting for transfers between devices: 1780 us -> 320 us  [the longest x2 134 us: local(): dos.append(lax.all_to_all(dob, 'eo', 0, 0, tiled=True))]
    reduce_scatter x0 -> x6, waiting for transfers between devices: none -> 401 us  [local(): lax.psum_scatter(g, 'ei', scatter_dimension=0, tiled=True)]
    dot_general x10 -> x0, matrix products: 217 us -> none  [the longest x1 42.4 us: local(): jnp.einsum('tkd,td->tk', oa, dy, preferred_element_type=jnp.float32)]
    all_to_all x0 -> x1, blocking collectives: none -> 194 us  [local(): lax.all_to_all(carry[0], 'eo', 0, 0, tiled=True).reshape(n_exp * cap, d)]
    pallas_call x0 -> x2, Pallas kernels: none -> 97.4 us  [_experts(): pl.pallas_call(functools.partial(_expert_kernel, 512), grid=(n_i,), in_sp...]
    all_to_all x6 -> x0, local copies, waits for them, and re-layouts: 83.2 us -> none  [the longest x2 27.8 us: to_experts(): r = lax.all_to_all(r, 'eo', 1, 1, tiled=True)]
    reduce_sum x2 -> x1, other arithmetic: 98.2 us -> 17.3 us  [local(): dgs.append(jnp.sum(dyf * oj, axis=1))]
    reshape x5, local copies, waits for them, and re-layouts: 80.4 us -> 3.37 us  [the longest x1 2.08 us: local(): jnp.zeros((nk + 1,), jnp.int32).at[flat]]
  transfers between devices with their start and end apart: 8 -> 17, of which waited for: 7 -> 9; matrix products, arithmetic and copies ran while one was open for 17% -> 25% of each run, Pallas kernels for 0% -> 3%
where the time goes in v1:
time: 1440 us
  waiting for transfers between devices  732 us (51%)
  local copies, waits for them, and re-layouts  311 us (22%)
  blocking collectives  194 us (13%)
  Pallas kernels  97.4 us (7%)
  other arithmetic  55.5 us (4%)
  starting transfers between devices  30.8 us (2%)
  between operations  14.9 us (1%)
    reduce_scatter x6, waiting for transfers between devices, local(): lax.psum_scatter(g, 'ei', scatter_dimension=0, tiled=True)  401 us
    all_to_all x1, blocking collectives, local(): lax.all_to_all(carry[0], 'eo', 0, 0, tiled=True).reshape(n_exp * cap, d)  194 us
    all_to_all x2, waiting for transfers between devices, local(): dos.append(lax.all_to_all(dob, 'eo', 0, 0, tiled=True))  134 us
    all_to_all x2, waiting for transfers between devices, local(): xs.append(lax.all_to_all(xb, 'eo', 0, 0, tiled=True))  102 us
    pallas_call x2, Pallas kernels, _experts(): pl.pallas_call(functools.partial(_expert_kernel, 512), grid=(n_i,), in_sp...  97.4 us
    all_to_all x1, waiting for transfers between devices, local(): lax.all_to_all(carry[1], 'eo', 0, 0, tiled=True).reshape(n_exp * cap, d)  84.5 us
    gather x2, local copies, waits for them, and re-layouts, local(): oj = ob[pos[:, j]].astype(F32)  57.6 us
    gather x2, local copies, waits for them, and re-layouts, local(): dx = dx + dxb[pos[:, j]].astype(F32)  57.5 us
  transfers between devices with their start and end apart: 17, of which 9 were waited for; matrix products, arithmetic and copies ran while one was open for 25% of the time, Pallas kernels for 3%

profile of v1, /device:TPU:0, one launch (start us, length us, event | category | flops | bytes accessed | tf_op | source)
XLA Modules:
  0.0 1435.3 jit_solution(1966450693653721563)
XLA Ops:
  7.2 3.0 fusion.11
  10.3 3.0 fusion.10
  13.4 0.7 copy.49
  14.1 1.2 reshape.243
  15.3 0.7 compare_select_fusion
  16.0 45.5 %gather_fusion.1 = f32[8192]{0:T(1024)S(1)} fusion(f32[8192]{0:T(1024)S(1)} %reshape.243, s32[8192]{0:T(1024)S(1)} %broadcast_clamp_fusion), kind=kCustom, calls=%fused_computation.1 | custom fusion | bytes 98304 | tf_op jit(solution)/shard_map/gather | solution.py:93
  61.7 25.2 %gather_fusion.4 = bf16[4096,1024]{1,0:T(8,128)(2,1)} fusion(bf16[4096,1024]{1,0:T(8,128)(2,1)} %param.13, s32[4096]{0:T(1024)S(1)} %broadcast_clamp_fusion.3), kind=kCustom, calls=%fused_computation.4 | custom fusion | bytes 16793600 | tf_op jit(solution)/shard_map/gather | solution.py:101
  87.0 8.2 fusion.4
  95.2 5.7 all-to-all-start.3
  101.0 1.5 fusion.9
  102.6 25.3 %gather_fusion.3 = bf16[4096,1024]{1,0:T(8,128)(2,1)} fusion(bf16[4096,1024]{1,0:T(8,128)(2,1)} %param.7, s32[4096]{0:T(1024)S(1)} %broadcast_clamp_fusion.3), kind=kCustom, calls=%fused_computation.3 | custom fusion | bytes 16793600 | tf_op jit(solution)/shard_map/gather | solution.py:99
  127.8 66.7 %all-to-all-done.3.do_ref = bf16[4,4,256,1024]{3,2,1,0:T(8,128)(2,1)} async-done(((bf16[4,4,256,1024]{3,2,1,0:T(8,128)(2,1)}), bf16[4,4,256,1024]{3,2,1,0:T(8,128)(2,1)}, u32[]{:S(2)}, u32[]{:S(2)}) %all-to-all-start.3) | async-done | bytes 8388640 | tf_op jit(solution)/shard_map/all_to_all | solution.py:102
  194.5 5.7 all-to-all-start.2
  200.9 25.2 %gather_fusion.2 = bf16[4096,1024]{1,0:T(8,128)(2,1)} fusion(bf16[4096,1024]{1,0:T(8,128)(2,1)} %param.13, s32[4096]{0:T(1024)S(1)} %broadcast_clamp_fusion.4), kind=kCustom, calls=%fused_computation.2 | custom fusion | bytes 16793600 | tf_op jit(solution)/shard_map/gather | solution.py:101
  226.2 8.2 fusion.5
  234.4 58.7 %all-to-all-done.2.x_ref = bf16[4,4,256,1024]{3,2,1,0:T(8,128)(2,1)} async-done(((bf16[4,4,256,1024]{3,2,1,0:T(8,128)(2,1)}), bf16[4,4,256,1024]{3,2,1,0:T(8,128)(2,1)}, u32[]{:S(2)}, u32[]{:S(2)}) %all-to-all-start.2) | async-done | bytes 8388640 | tf_op jit(solution)/shard_map/all_to_all | solution.py:100
  293.0 5.7 all-to-all-start.1
  299.3 25.2 %gather_fusion = bf16[4096,1024]{1,0:T(8,128)(2,1)} fusion(bf16[4096,1024]{1,0:T(8,128)(2,1)} %param.7, s32[4096]{0:T(1024)S(1)} %broadcast_clamp_fusion.4), kind=kCustom, calls=%fused_computation | custom fusion | bytes 16793600 | tf_op jit(solution)/shard_map/gather | solution.py:99
  324.6 67.0 %all-to-all-done.1.do_ref = bf16[4,4,256,1024]{3,2,1,0:T(8,128)(2,1)} async-done(((bf16[4,4,256,1024]{3,2,1,0:T(8,128)(2,1)}), bf16[4,4,256,1024]{3,2,1,0:T(8,128)(2,1)}, u32[]{:S(2)}, u32[]{:S(2)}) %all-to-all-start.1) | async-done | bytes 8388640 | tf_op jit(solution)/shard_map/all_to_all | solution.py:102
  391.5 5.6 all-to-all-start
  398.3 48.6 %experts0.1 = (bf16[4,2,4,256,1024]{4,3,2,1,0:T(8,128)(2,1)}, bf16[4,2,4,256,1024]{4,3,2,1,0:T(8,128)(2,1)}, f32[4,1024,512]{2,1,0:T(8,128)}, f32[4,1024,512]{2,1,0:T(8,128)}, f32[4,512,1024]{2,1,0:T(8,128)}) custom-call(bf16[4,4,256,1024]{3,2,1,0:T(8,128)(2,1)} %all-to-all-done.2.x_ref, bf16[4,4,256,1024]{3,2,1,0:T(8,128)(2,1)} %all-to-all-done.3.do_ref, ...), custom_call_target="tpu_custom_call" | custom-call | flops 38654705664 | bytes 71303168 | tf_op jit(solution)/shard_map/experts0/pallas_call | solution.py:62
  446.9 43.1 %all-to-all-done.x_ref = bf16[4,4,256,1024]{3,2,1,0:T(8,128)(2,1)} async-done(((bf16[4,4,256,1024]{3,2,1,0:T(8,128)(2,1)}), bf16[4,4,256,1024]{3,2,1,0:T(8,128)(2,1)}, u32[]{:S(2)}, u32[]{:S(2)}) %all-to-all-start) | async-done | bytes 8388640 | tf_op jit(solution)/shard_map/all_to_all | solution.py:100
  490.0 6.5 all-gather.9.cloned.1.call-done.w3_ref
  496.5 48.8 %experts1.1 = (bf16[4,2,4,256,1024]{4,3,2,1,0:T(8,128)(2,1)}, bf16[4,2,4,256,1024]{4,3,2,1,0:T(8,128)(2,1)}, f32[4,1024,512]{2,1,0:T(8,128)}, f32[4,1024,512]{2,1,0:T(8,128)}, f32[4,512,1024]{2,1,0:T(8,128)}) custom-call(bf16[4,4,256,1024]{3,2,1,0:T(8,128)(2,1)} %all-to-all-done.x_ref, ...), custom_call_target="tpu_custom_call", output_to_operand_aliasing={{0}: (5, {}), {1}: (6, {})} | custom-call | flops 38654705664 | bytes 71303168 | tf_op jit(solution)/shard_map/experts1/pallas_call | solution.py:62
  545.3 0.7 reduce-scatter.15.cloned.1.call-update
  546.1 0.7 reduce-scatter.13.cloned.1.call-update
  547.4 0.7 reduce-scatter.9.cloned.1.call-update
  548.1 193.8 %all_to_all.30 = bf16[4,2,4,256,1024]{4,3,2,1,0:T(8,128)(2,1)} all-to-all(bf16[4,2,4,256,1024]{4,3,2,1,0:T(8,128)(2,1)} %get-tuple-element.18), channel_id=1, replica_groups=mesh['dp'=2,'ei'=4,'eo'=4] {'eo'}, dimensions={0} | all-to-all | bytes 33554432 | tf_op jit(solution)/shard_map/all_to_all | solution.py:110
  741.9 7.0 all-to-all-start.5
  749.5 30.6 %scatter_custom_fusion = s32[8193]{0:T(1024)S(1)} fusion(s32[8192]{0:T(1024)} %bitcast.44, s32[8192]{0:T(1024)S(1)} %iota.3, s32[]{:T(128)} %constant.30.clone.1), kind=kCustom, calls=%fused_computation.43 | custom fusion | bytes 33284 | tf_op jit(solution)/shard_map/scatter | solution.py:113
  780.1 2.1 reshape.247
  782.2 2.7 fusion.8
  784.9 2.2 copy.53
  787.1 2.2 copy.52
  789.4 28.9 %gather_fusion.6 = bf16[4096,1024]{1,0:T(8,128)(2,1)} fusion(bf16[8192,1024]{1,0:T(8,128)(2,1)} %bitcast.27, s32[4096]{0:T(1024)S(1)} %broadcast_clamp_fusion.1), kind=kCustom, calls=%fused_computation.6 | custom fusion | bytes 16793600 | tf_op jit(solution)/shard_map/gather | solution.py:118
  818.3 28.7 %gather_fusion.5 = bf16[4096,1024]{1,0:T(8,128)(2,1)} fusion(bf16[8192,1024]{1,0:T(8,128)(2,1)} %bitcast.28, s32[4096]{0:T(1024)S(1)} %broadcast_clamp_fusion.2), kind=kCustom, calls=%fused_computation.5 | custom fusion | bytes 16793600 | tf_op jit(solution)/shard_map/gather | solution.py:118
  847.1 84.5 %all-to-all-done.5 = bf16[4,2,4,256,1024]{4,3,2,1,0:T(8,128)(2,1)} async-done(((bf16[4,2,4,256,1024]{4,3,2,1,0:T(8,128)(2,1)}), bf16[4,2,4,256,1024]{4,3,2,1,0:T(8,128)(2,1)}, u32[]{:S(2)}, u32[]{:S(2)}) %all-to-all-start.5) | async-done | bytes 16777248 | tf_op jit(solution)/shard_map/all_to_all | solution.py:111
  931.6 28.7 %gather_fusion.7 = bf16[4096,1024]{1,0:T(8,128)(2,1)} fusion(bf16[8192,1024]{1,0:T(8,128)(2,1)} %bitcast.16, s32[4096]{0:T(1024)S(1)} %broadcast_clamp_fusion.2), kind=kCustom, calls=%fused_computation.7 | custom fusion | bytes 16793600 | tf_op jit(solution)/shard_map/gather | solution.py:124
  960.3 28.7 %gather_fusion.8 = bf16[4096,1024]{1,0:T(8,128)(2,1)} fusion(bf16[8192,1024]{1,0:T(8,128)(2,1)} %bitcast.16, s32[4096]{0:T(1024)S(1)} %broadcast_clamp_fusion.1), kind=kCustom, calls=%fused_computation.8 | custom fusion | bytes 16793600 | tf_op jit(solution)/shard_map/gather | solution.py:124
  989.1 17.3 %fusion.2 = (f32[4096]{0:T(1024)S(1)}, f32[4096]{0:T(1024)S(1)}, bf16[4096,1024]{1,0:T(8,128)(2,1)}) fusion(bf16[4096,1024]{1,0:T(8,128)(2,1)} %gather_fusion.5, bf16[4096,1024]{1,0:T(8,128)(2,1)} %param.13, bf16[4096,1024]{1,0:T(8,128)(2,1)} %gather_fusion.6, f32[4096]{0:T(1024)S(1)} %bitcast.37, f32[4096]{0:T(1024)S(1)} %bitcast.36), kind=kLoop, calls=%fused_computation.16 | loop fusion | flops 46129152 | bytes 33619968 | tf_op jit(solution)/shard_map/reduce_sum | solution.py:120
  1006.4 0.6 pad_maximum_fusion.3
  1007.0 6.0 add_convert_fusion
  1013.0 4.8 pad_maximum_fusion.2
  1017.8 111.6 %reduce-scatter.11.cloned.1.call-done = f32[1,1024,512]{2,1,0:T(8,128)} async-done(((f32[4,1024,512]{2,1,0:T(8,128)}), f32[1,1024,512]{2,1,0:T(8,128)}) %reduce-scatter.11.cloned.1.call-update) | async-done | bytes 2097168 | tf_op jit(solution)/shard_map/reduce_scatter | solution.py:109
  1129.4 4.7 pad_maximum_fusion.1
  1134.0 142.4 %reduce-scatter.9.cloned.1.call-done = f32[1,1024,512]{2,1,0:T(8,128)} async-done(((f32[4,1024,512]{2,1,0:T(8,128)}), f32[1,1024,512]{2,1,0:T(8,128)}) %reduce-scatter.9.cloned.1.call-update) | async-done | bytes 2097168 | tf_op jit(solution)/shard_map/reduce_scatter | solution.py:109
  1276.4 146.9 %reduce-scatter.7.cloned.1.call-done = f32[1,1024,512]{2,1,0:T(8,128)} async-done(((f32[4,1024,512]{2,1,0:T(8,128)}), f32[1,1024,512]{2,1,0:T(8,128)}) %reduce-scatter.7.cloned.1.call-update) | async-done | bytes 2097168 | tf_op jit(solution)/shard_map/reduce_scatter | solution.py:109
  1423.3 4.7 pad_maximum_fusion
  (62 shorter events, 4.2 us)
Async XLA Ops:
  7.2 6.2 copy-start.5
  7.2 6.3 copy-start.3
  7.2 391.0 %all-gather.13.cloned.1.call-start = ((), (), s32[]{:S(2)}) async-start(), calls=%async_computation.15 | async-start | bytes 5242880 | tf_op jit(solution)/shard_map/all_gather | solution.py:103
  10.2 388.0 %all-gather.15.cloned.1.call-start = ((), (), s32[]{:S(2)}) async-start(), calls=%async_computation.16 | async-start | bytes 5242880 | tf_op jit(solution)/shard_map/all_gather | solution.py:103
  95.2 5.8 copy-start.2
  95.2 99.3 %all-to-all-start.3 = ((bf16[4,4,256,1024]{3,2,1,0:T(8,128)(2,1)}), bf16[4,4,256,1024]{3,2,1,0:T(8,128)(2,1)}, u32[]{:S(2)}, u32[]{:S(2)}) async-start(bf16[4,4,256,1024]{3,2,1,0:T(8,128)(2,1)} %fusion.4), calls=%async_computation.3 | async-start | bytes 16777216 | tf_op jit(solution)/shard_map/all_to_all | solution.py:102
  101.0 297.3 %all-gather.17.cloned.1.call-start = ((), (), s32[]{:S(2)}) async-start(), calls=%async_computation.17 | async-start | bytes 5242880 | tf_op jit(solution)/shard_map/all_gather | solution.py:103
  194.5 98.5 %all-to-all-start.2 = ((bf16[4,4,256,1024]{3,2,1,0:T(8,128)(2,1)}), bf16[4,4,256,1024]{3,2,1,0:T(8,128)(2,1)}, u32[]{:S(2)}, u32[]{:S(2)}) async-start(bf16[4,4,256,1024]{3,2,1,0:T(8,128)(2,1)} %bitcast.32), calls=%async_computation.2 | async-start | bytes 16777216 | tf_op jit(solution)/shard_map/all_to_all | solution.py:100
  200.2 289.8 %all-gather.11.cloned.1.call-start = ((), (), s32[]{:S(2)}) async-start(), calls=%async_computation.14 | async-start | bytes 5242880 | tf_op jit(solution)/shard_map/all_gather | solution.py:103
  293.0 98.5 %all-to-all-start.1 = ((bf16[4,4,256,1024]{3,2,1,0:T(8,128)(2,1)}), bf16[4,4,256,1024]{3,2,1,0:T(8,128)(2,1)}, u32[]{:S(2)}, u32[]{:S(2)}) async-start(bf16[4,4,256,1024]{3,2,1,0:T(8,128)(2,1)} %fusion.5), calls=%async_computation.1 | async-start | bytes 16777216 | tf_op jit(solution)/shard_map/all_to_all | solution.py:102
  298.7 191.3 %all-gather.7.cloned.1.call-start = ((), (), s32[]{:S(2)}) async-start(), calls=%async_computation.12 | async-start | bytes 5242880 | tf_op jit(solution)/shard_map/all_gather | solution.py:103
  391.5 98.4 %all-to-all-start = ((bf16[4,4,256,1024]{3,2,1,0:T(8,128)(2,1)}), bf16[4,4,256,1024]{3,2,1,0:T(8,128)(2,1)}, u32[]{:S(2)}, u32[]{:S(2)}) async-start(bf16[4,4,256,1024]{3,2,1,0:T(8,128)(2,1)} %bitcast.31), calls=%async_computation | async-start | bytes 16777216 | tf_op jit(solution)/shard_map/all_to_all | solution.py:100
  397.2 99.3 %all-gather.9.cloned.1.call-start = ((), (), s32[]{:S(2)}) async-start(), calls=%async_computation.13 | async-start | bytes 5242880 | tf_op jit(solution)/shard_map/all_gather | solution.py:103
  397.7 615.2 %reduce-scatter.17.cloned.1.call-start = ((), (), s32[]{:S(2)}) async-start(), calls=%async_computation.23 | async-start | bytes 10485760 | tf_op jit(solution)/shard_map/reduce_scatter | solution.py:109
  545.3 467.7 %reduce-scatter.15.cloned.1.call-start = ((), (), s32[]{:S(2)}) async-start(), calls=%async_computation.22 | async-start | bytes 10485760 | tf_op jit(solution)/shard_map/reduce_scatter | solution.py:109
  546.0 471.8 %reduce-scatter.13.cloned.1.call-start = ((), (), s32[]{:S(2)}) async-start(), calls=%async_computation.21 | async-start | bytes 10485760 | tf_op jit(solution)/shard_map/reduce_scatter | solution.py:109
  546.8 582.6 %reduce-scatter.11.cloned.1.call-start = ((), (), s32[]{:S(2)}) async-start(), calls=%async_computation.20 | async-start | bytes 10485760 | tf_op jit(solution)/shard_map/reduce_scatter | solution.py:109
  547.4 729.1 %reduce-scatter.9.cloned.1.call-start = ((), (), s32[]{:S(2)}) async-start(), calls=%async_computation.19 | async-start | bytes 10485760 | tf_op jit(solution)/shard_map/reduce_scatter | solution.py:109
  741.9 189.7 %all-to-all-start.5 = ((bf16[4,2,4,256,1024]{4,3,2,1,0:T(8,128)(2,1)}), bf16[4,2,4,256,1024]{4,3,2,1,0:T(8,128)(2,1)}, u32[]{:S(2)}, u32[]{:S(2)}) async-start(bf16[4,2,4,256,1024]{4,3,2,1,0:T(8,128)(2,1)} %get-tuple-element.19), calls=%async_computation.5 | async-start | bytes 33554432 | tf_op jit(solution)/shard_map/all_to_all | solution.py:111
  748.9 674.5 %reduce-scatter.7.cloned.1.call-start = ((), (), s32[]{:S(2)}) async-start(), calls=%async_computation.18 | async-start | bytes 10485760 | tf_op jit(solution)/shard_map/reduce_scatter | solution.py:109
  749.5 39.9 %copy-start.4 = (f32[4096,2]{0,1:T(2,128)S(1)}, f32[4096,2]{0,1:T(2,128)}, u32[]{:S(2)}) copy-start(f32[4096,2]{0,1:T(2,128)} %param.9) | copy-start | bytes 98308
  989.0 18.0 %copy-start = (bf16[4096,1024]{1,0:T(8,128)(2,1)S(1)}, bf16[4096,1024]{1,0:T(8,128)(2,1)}, u32[]{:S(2)}) copy-start(bf16[4096,1024]{1,0:T(8,128)(2,1)} %gather_fusion.7) | copy-start | bytes 25165828
  989.1 18.0 %copy-start.1 = (bf16[4096,1024]{1,0:T(8,128)(2,1)S(1)}, bf16[4096,1024]{1,0:T(8,128)(2,1)}, u32[]{:S(2)}) copy-start(bf16[4096,1024]{1,0:T(8,128)(2,1)} %gather_fusion.8) | copy-start | bytes 25165828
Sparse Core Ops, SparseCore 0:
  10.4 82.9 all-gather.12
  95.5 78.8 all-gather.14
  176.0 78.8 all-gather.16
  256.3 78.8 all-gather.10
  337.2 78.8 all-gather.6
  417.5 78.8 all-gather.8
  545.4 142.8 reduce-scatter.16
  690.7 144.6 reduce-scatter.14
  837.8 144.6 reduce-scatter.12
  984.7 144.6 reduce-scatter.10
  1131.7 144.6 reduce-scatter.8
  1278.6 144.6 reduce-scatter.6
